TPU v7x, 32 devices: a whole 2x2x4 slice. The times are simulated.
32 devices in a mesh: seq: 8 (over y, x, core), head: 4 (over z).
Axes of the slice: x: 2, y: 2, z: 4, core: 2. Of those that a mesh axis runs over, the one named last changes fastest.
Arguments:
- queries: bfloat16 [1024, 1024], P('seq', 'head'), may hold values from -24 to 24
- keys_values: bfloat16 [2, 1024, 128], P(None, 'seq'), may hold values from -6 to 6
- out_weight: bfloat16 [2560, 8, 128], P('head'), may hold values from -0.125 to 0.125
- out_grad: bfloat16 [1024, 2560], P('seq'), may hold values from -6 to 6
- positions: int32 [1024], replicated, may hold values from 0 to 1023, as said below
Outputs:
- d_query: bfloat16 [1024, 1024], P('seq', 'head')
- d_out_weight: float32 [2560, 8, 128], P('seq', 'head')
Inputs may be any that keep to these rules, and one draw needn't show every extreme that they name: positions holds each of 0 to 1023 once, in runs of 64 consecutive rows with consecutive positions, each run starting at a row and a position that are multiples of 64.
All inputs are finite; a program needn't handle non-finite values.
Results may differ from a plain program's by a relative error of at most 0.007.
Values may be sent and summed in bfloat16 or wider, within the bound.
A program may use at most 64 MiB of HBM per device.

v0:
```python
import math

import jax
import jax.numpy as jnp
from jax import lax
from jax.sharding import PartitionSpec as P

HD = 128
GROUP = 8


big_negative = -1e30


def attend_block(query_rows, query_pos, block_kv, key_pos, scale):
    scores = (
        lax.dot_general(
            query_rows, block_kv[0], (((1,), (1,)), ((), ())), preferred_element_type=jnp.float32
        )
        * scale
    )
    visible = key_pos[None, :] <= query_pos[:, None]
    return (jnp.where(visible, scores, big_negative), visible)


def sweep(step_fn, states, key_piece, offset, positions):
    span_size = key_piece.shape[1]
    block_size = math.gcd(span_size, 1024)

    def step(step_index, inner):
        block_kv = lax.dynamic_slice_in_dim(key_piece, step_index * block_size, block_size, 1)
        key_pos = lax.dynamic_slice_in_dim(
            positions, offset + step_index * block_size, block_size, 0
        )
        return step_fn(inner, block_kv, key_pos)

    return lax.fori_loop(0, span_size // block_size, step, states)


def body(queries, keys_values, out_weight, out_grad, positions):
    token_count = queries.shape[0]
    head_count = queries.shape[1] // HD
    scale = HD ** (-0.5)
    seq_index = lax.axis_index("seq")
    head_index = lax.axis_index("head")
    kv_group = head_index * head_count // GROUP
    own_kv = lax.dynamic_slice_in_dim(keys_values, kv_group * HD, HD, 2)
    own_pos = lax.dynamic_slice_in_dim(positions, seq_index * token_count, token_count, 0)
    query_pos = jnp.repeat(own_pos, head_count)
    query_rows = queries.reshape(token_count * head_count, HD)
    d_attn = jnp.einsum(
        "td,dhc->thc",
        out_grad,
        lax.all_to_all(out_weight, "head", split_axis=1, concat_axis=0, tiled=True),
        preferred_element_type=jnp.float32,
    )
    d_attn = d_attn.astype(jnp.bfloat16).reshape(token_count * head_count, HD)
    row_total = token_count * head_count
    zeros_col = jnp.zeros((row_total, 1), jnp.float32)
    zeros_rows = jnp.zeros((row_total, HD), jnp.float32)
    lowest_col = jnp.full((row_total, 1), big_negative, jnp.float32)
    all_kv = lax.all_gather(own_kv, "seq", axis=1, tiled=True)

    def run_sweep(step_fn, init):
        return sweep(step_fn, init, all_kv, 0, positions)

    def stats_step(states, block_kv, key_pos):
        top, norm = states
        scores, visible = attend_block(query_rows, query_pos, block_kv, key_pos, scale)
        new_top = jnp.maximum(top, jnp.max(scores, axis=1, keepdims=True))
        weights = jnp.where(visible, jnp.exp(scores - new_top), 0.0)
        norm = jnp.exp(top - new_top) * norm + jnp.sum(weights, axis=1, keepdims=True)
        return (new_top, norm)

    top, norm = run_sweep(stats_step, (lowest_col, zeros_col))

    def block_probs(block_kv, key_pos):
        scores, visible = attend_block(query_rows, query_pos, block_kv, key_pos, scale)
        return jnp.where(visible, jnp.exp(scores - top), 0.0) / norm

    def out_step(acc_out, block_kv, key_pos):
        probs = block_probs(block_kv, key_pos)
        return acc_out + jnp.dot(
            probs.astype(jnp.bfloat16), block_kv[1], preferred_element_type=jnp.float32
        )

    attn_full = run_sweep(out_step, zeros_rows)
    delta = jnp.sum(d_attn.astype(jnp.float32) * attn_full, axis=1, keepdims=True)

    def grad_step(acc_grad, block_kv, key_pos):
        probs = block_probs(block_kv, key_pos)
        dprob = lax.dot_general(
            d_attn, block_kv[1], (((1,), (1,)), ((), ())), preferred_element_type=jnp.float32
        )
        dscore = (probs * (dprob - delta)).astype(jnp.bfloat16)
        return acc_grad + jnp.dot(dscore, block_kv[0], preferred_element_type=jnp.float32)

    d_rows = run_sweep(grad_step, zeros_rows) * scale
    attn = attn_full.astype(jnp.bfloat16).reshape(token_count, head_count, HD)
    d_query = d_rows.astype(jnp.bfloat16).reshape(token_count, head_count * HD)
    d_out_weight = lax.psum_scatter(
        jnp.einsum("td,thc->dhc", out_grad, attn, preferred_element_type=jnp.float32),
        "seq",
        scatter_dimension=0,
        tiled=True,
    )
    return (d_query, d_out_weight)


def solution(mesh):
    return jax.shard_map(
        body,
        mesh=mesh,
        in_specs=(
            P("seq", "head"),
            P(None, "seq", None),
            P("head", None, None),
            P("seq", None),
            P(),
        ),
        out_specs=(P("seq", "head"), P("seq", "head", None)),
        check_vma=False,
    )
```

profile of v0, /device:TPU:1, one launch (start us, length us, event | category | flops | bytes accessed | tf_op | source)
XLA Modules:
  0.0 123.6 jit_solution(11164809730574350599)
XLA Ops:
  7.2 2.6 %copy.14 = bf16[640,8,128]{2,0,1:T(8,128)(2,1)} copy(bf16[640,8,128]{2,1,0:T(8,128)(2,1)} %param.7) | data formatting | bytes 2621440 | tf_op args[2]
  9.8 5.5 %all-to-all-start = ((bf16[640,8,128]{2,0,1:T(8,128)(2,1)}), bf16[640,8,128]{2,0,1:T(8,128)(2,1)S(1)}, u32[]{:S(2)}, u32[]{:S(2)}) async-start(bf16[640,8,128]{2,0,1:T(8,128)(2,1)} %copy.14), calls=%async_computation | async-start | bytes 2621440 | tf_op jit(solution)/shard_map/all_to_all | solution.py:54
  15.4 0.1 dynamic_slice.16
  15.5 0.1 broadcast_in_dim.38
  15.6 0.1 le.51
  15.7 10.7 %all_gather.3 = bf16[2,1024,128]{2,1,0:T(8,128)(2,1)S(1)} all-gather(bf16[2,128,128]{2,1,0:T(8,128)(2,1)S(1)} %copy-done.7), channel_id=1, replica_groups=mesh['seq'=8,'head'=4] {'seq'}, dimensions={1}, use_global_device_ids=true | all-gather | bytes 589824 | tf_op jit(solution)/shard_map/all_gather | solution.py:62
  26.4 0.4 fusion.15
  26.8 0.4 fusion.7
  27.2 0.3 fusion.6
  27.5 18.8 %all-to-all-done = bf16[640,8,128]{2,0,1:T(8,128)(2,1)S(1)} async-done(((bf16[640,8,128]{2,0,1:T(8,128)(2,1)}), bf16[640,8,128]{2,0,1:T(8,128)(2,1)S(1)}, u32[]{:S(2)}, u32[]{:S(2)}) %all-to-all-start) | async-done | bytes 1310752 | tf_op jit(solution)/shard_map/all_to_all | solution.py:54
  46.3 0.1 copy.15
  46.4 0.4 convolution_convert_fusion
  46.7 0.1 copy.16
  46.8 0.4 fusion.14
  47.2 0.2 copy-done.5
  47.4 0.5 convolution_bitcast_fusion
  48.0 3.1 %copy.18 = f32[2560,2,128]{2,1,0:T(2,128)} copy(f32[2560,2,128]{0,2,1:T(8,128)S(1)} %convolution_bitcast_fusion) | data formatting | bytes 5242880 | tf_op jit(solution)/shard_map/td,thc->dhc/dot_general | solution.py:102
  51.1 0.0 all-reduce.3.cloned.1.call-update
  51.1 0.6 copy-done.10
  51.8 0.6 dynamic-slice
  53.0 0.4 fusion.5
  53.5 0.7 reshape.37
  54.1 60.9 %all-reduce.3.cloned.1.call-done = f32[2560,2,128]{2,1,0:T(2,128)} async-done(((f32[2560,2,128]{2,1,0:T(2,128)}), f32[2560,2,128]{2,1,0:T(2,128)}) %all-reduce.3.cloned.1.call-update) | async-done | bytes 2621456
  115.0 1.7 %constant_dynamic-slice_fusion = f32[320,2,128]{2,1,0:T(2,128)} fusion(f32[2560,2,128]{2,1,0:T(2,128)} %all-reduce.3.cloned.1.call-done, u32[]{:T(128)S(6)} %multiply.1), kind=kLoop, calls=%fused_computation.23 | loop fusion | bytes 655364
  (24 shorter events, 0.1 us)
Async XLA Ops:
  7.2 39.2 %copy-start = (bf16[128,2560]{1,0:T(8,128)(2,1)S(1)}, bf16[128,2560]{1,0:T(8,128)(2,1)}, u32[]{:S(2)}) copy-start(bf16[128,2560]{1,0:T(8,128)(2,1)} %param.8) | copy-start | bytes 1966084
  9.8 5.6 %copy-start.8 = (bf16[128,256]{1,0:T(8,128)(2,1)S(1)}, bf16[128,256]{1,0:T(8,128)(2,1)}, u32[]{:S(2)}) copy-start(bf16[128,256]{1,0:T(8,128)(2,1)} %param.5) | copy-start | bytes 196612
  9.8 5.6 %copy-start.9 = (s32[1024]{0:T(1024)S(1)}, s32[1024]{0:T(1024)}, u32[]{:S(2)}) copy-start(s32[1024]{0:T(1024)} %param.9) | copy-start | bytes 12292
  9.8 5.9 %copy-start.7 = (bf16[2,128,128]{2,1,0:T(8,128)(2,1)S(1)}, bf16[2,128,128]{2,1,0:T(8,128)(2,1)}, u32[]{:S(2)}) copy-start(bf16[2,128,128]{2,1,0:T(8,128)(2,1)} %param.6) | copy-start | bytes 196612
  9.8 36.4 %all-to-all-start = ((bf16[640,8,128]{2,0,1:T(8,128)(2,1)}), bf16[640,8,128]{2,0,1:T(8,128)(2,1)S(1)}, u32[]{:S(2)}, u32[]{:S(2)}) async-start(bf16[640,8,128]{2,0,1:T(8,128)(2,1)} %copy.14), calls=%async_computation | async-start | bytes 2621440 | tf_op jit(solution)/shard_map/all_to_all | solution.py:54
  15.4 99.7 %all-reduce.3.cloned.1.call-start = ((), (), s32[]{:S(2)}) async-start(), calls=%async_computation.1 | async-start | bytes 5242880
  26.4 20.4 %copy-start.3 = (bf16[2,1024,128]{2,1,0:T(8,128)(2,1)}, bf16[2,1024,128]{2,1,0:T(8,128)(2,1)S(1)}, u32[]{:S(2)}) copy-start(bf16[2,1024,128]{2,1,0:T(8,128)(2,1)S(1)} %all_gather.3) | copy-start | bytes 1572868
  27.5 19.3 %copy-start.1 = (f32[256,1024]{1,0:T(8,128)}, f32[256,1024]{1,0:T(8,128)S(1)}, u32[]{:S(2)}) copy-start(f32[256,1024]{1,0:T(8,128)S(1)} %fusion.6) | copy-start | bytes 3145732
  46.8 0.6 copy-start.5
  51.1 0.7 copy-start.10
  51.1 1.9 %copy-start.2 = (f32[256,1024]{1,0:T(8,128)S(1)}, f32[256,1024]{1,0:T(8,128)}, u32[]{:S(2)}) copy-start(f32[256,1024]{1,0:T(8,128)} %copy-done.1) | copy-start | bytes 3145732
  51.1 1.9 %copy-start.4 = (bf16[2,1024,128]{2,1,0:T(8,128)(2,1)S(1)}, bf16[2,1024,128]{2,1,0:T(8,128)(2,1)}, u32[]{:S(2)}) copy-start(bf16[2,1024,128]{2,1,0:T(8,128)(2,1)} %copy-done.3) | copy-start | bytes 1572868
  51.1 1.9 %copy-start.6 = (bf16[128,2,128]{2,1,0:T(2,128)(2,1)S(1)}, bf16[128,2,128]{2,1,0:T(2,128)(2,1)}, u32[]{:S(2)}) copy-start(bf16[128,2,128]{2,1,0:T(2,128)(2,1)} %copy-done.5) | copy-start | bytes 196612
Sparse Core Ops, SparseCore 0:
  51.3 63.7 all-reduce.2
where the time goes:
time: 125 us; the launch traced here: 124 us
  waiting for transfers between devices  79.7 us (64%)
  between operations  14.8 us (12%)
  blocking collectives  10.7 us (9%)
  local copies, waits for them, and re-layouts  10.1 us (8%)
  starting transfers between devices  5.54 us (4%)
  matrix products  2.08 us (2%)
    unnamed x2, waiting for transfers between devices  60.9 us
    all_to_all x1, waiting for transfers between devices, body(): lax.all_to_all(out_weight, 'head', split_axis=1, concat_axis=0, tiled=True)  18.8 us
    all_gather x1, blocking collectives, body(): all_kv = lax.all_gather(own_kv, 'seq', axis=1, tiled=True)  10.7 us
    unnamed x25, local copies, waits for them, and re-layouts  5.82 us
    all_to_all x1, starting transfers between devices, body(): lax.all_to_all(out_weight, 'head', split_axis=1, concat_axis=0, tiled=True)  5.54 us
    dot_general x1, local copies, waits for them, and re-layouts, body(): jnp.einsum('td,thc->dhc', out_grad, attn, preferred_element_type=jnp.floa...  3.14 us
  transfers between devices with their start and end apart: 2, of which 2 were waited for; matrix products, arithmetic and copies ran while one was open for 3% of the time, Pallas kernels for 0%

commit v1 on v0

v1 whole, which is shorter than its diff:
```python
import functools

import jax
import jax.numpy as jnp
from jax import lax
from jax.experimental import pallas as pl
from jax.experimental.pallas import tpu as pltpu
from jax.sharding import PartitionSpec as P

HD = 128
GROUP = 8
RUN = 64
BIG_NEGATIVE = -1e30
MESH = pl.DeviceIdType.MESH


def remote(src, dst, send_sem, recv_sem, axis, peer):
    return pltpu.make_async_remote_copy(
        src_ref=src,
        dst_ref=dst,
        send_sem=send_sem,
        recv_sem=recv_sem,
        device_id={axis: peer},
        device_id_type=MESH,
    )


class Gather:
    def __init__(self, n, me, own, slots, send, relay, recv):
        self.n, self.me, self.own, self.slots = n, me, own, slots
        self.send, self.relay, self.recv = send, relay, recv
        self.core = lax.rem(me, 2)
        self.half = lax.div(me, 2)
        self.partner = me + 1 - 2 * self.core

    def peer(self, k):
        return 2 * lax.rem(self.half + k, self.n // 2) + self.core

    def copies(self):
        for k in range(self.n // 2):
            to = self.partner if k == 0 else self.peer(k)
            yield remote(
                self.own, self.slots.at[self.me], self.send.at[k], self.recv.at[self.me], "seq", to
            )

    def relay_copy(self, k):
        src = self.peer(k)
        return remote(
            self.slots.at[src],
            self.slots.at[src],
            self.relay.at[k],
            self.recv.at[src],
            "seq",
            self.partner,
        )

    def start(self):
        for copy in self.copies():
            copy.start()

    def arrived(self, src):
        remote(
            self.own, self.slots.at[src], self.send.at[0], self.recv.at[src], "seq", self.partner
        ).wait_recv()

    def pass_on(self, k):
        self.arrived(self.peer(k))
        self.relay_copy(k).start()

    def other(self, k):
        return self.peer(k) + 1 - 2 * self.core

    def finish(self):
        for copy in self.copies():
            copy.wait_send()
        for k in range(1, self.n // 2):
            self.relay_copy(k).wait_send()


def kernel(
    n,
    m,
    turn,
    pos_ref,
    q_ref,
    kv_ref,
    g_hbm,
    w_hbm,
    dq_ref,
    dw_ref,
    g_v,
    gt_v,
    w_v,
    kv_all,
    part,
    part_own,
    part_all,
    attn_own,
    attn_all,
    g_all,
    scores,
    local_sem,
    kv_send,
    kv_relay,
    kv_recv,
    at_send,
    at_relay,
    at_recv,
    g_send,
    g_recv,
    p_send,
    p_recv,
):
    me = lax.axis_index("seq")
    hme = lax.axis_index("head")
    tok = q_ref.shape[0]
    heads = q_ref.shape[1] // HD
    rows = g_all.shape[1]
    dz = w_v.shape[0]
    scale = HD ** (-0.5)

    g_copy = pltpu.make_async_copy(g_hbm, g_v, local_sem.at[0])
    w_copy = pltpu.make_async_copy(w_hbm, w_v, local_sem.at[1])
    g_copy.start()
    w_copy.start()

    barrier = pltpu.get_barrier_semaphore()
    for k in range(1, n):
        pl.semaphore_signal(
            barrier, inc=1, device_id={"seq": lax.rem(me + k, n)}, device_id_type=MESH
        )
    for k in range(1, m):
        pl.semaphore_signal(
            barrier, inc=1, device_id={"head": lax.rem(hme + k, m)}, device_id_type=MESH
        )
    pl.semaphore_wait(barrier, n + m - 2)

    group = lax.div(hme * heads, GROUP)
    columns = pl.ds(pl.multiple_of(group * HD, HD), HD)
    own_kv = kv_ref.at[:, :, columns]
    kv = Gather(n, me, own_kv, kv_all, kv_send, kv_relay, kv_recv)
    kv.start()
    kv_all[me] = own_kv[...]

    g_copy.wait()
    if turn:
        for j in range(n * rows // HD):
            gt_v[pl.ds(j * HD, HD), :] = g_v[:, pl.ds(j * HD, HD)].T

        def g_block(i):
            return gt_v.at[pl.ds(pl.multiple_of(i * rows, 16), rows)]

    else:

        def g_block(i):
            return g_v.at[i]

    def g_send_copy(k):
        to = lax.rem(me + k, n)
        return remote(g_block(to), g_all.at[me], g_send.at[k], g_recv.at[me], "seq", to)

    for k in range(1, n):
        g_send_copy(k).start()

    w_copy.wait()

    def partial(j):
        wide = heads * HD
        total = jnp.zeros((tok, wide), jnp.float32)
        if turn:
            lhs = g_v[:, pl.ds(pl.multiple_of(hme * dz, HD), dz)]
            for h in range(heads):
                piece = jnp.dot(
                    lhs, w_v[:, j * heads + h, :], preferred_element_type=jnp.float32
                )
                yield piece
        else:
            blocks = dz // rows
            for h in range(heads):
                total = jnp.zeros((tok, HD), jnp.float32)
                for b in range(blocks):
                    total = total + lax.dot_general(
                        g_v[hme * blocks + b],
                        w_v[pl.ds(b * rows, rows), j * heads + h, :],
                        (((0,), (0,)), ((), ())),
                        preferred_element_type=jnp.float32,
                    )
                yield total

    for j in range(m):
        for h, piece in enumerate(partial(j)):
            part[j, :, pl.ds(h * HD, HD)] = piece.astype(jnp.bfloat16)

    def p_copy(k):
        to = lax.rem(hme + k, m)
        return remote(part.at[to], part_all.at[hme], p_send.at[k], p_recv.at[hme], "head", to)

    for k in range(1, m):
        p_copy(k).start()

    for k in range(1, n // 2):
        kv.pass_on(k)
    for k in range(n // 2):
        kv.arrived(kv.other(k))

    query = jnp.concatenate([q_ref[:, pl.ds(h * HD, HD)] for h in range(heads)], axis=0)
    total_rows = heads * tok
    row = lax.broadcasted_iota(jnp.int32, (tok, 1), 0)
    lane = lax.broadcasted_iota(jnp.int32, (1, tok), 1)

    def run_positions(block, index):
        value = pos_ref[block * tok] + index
        for r in range(1, tok // RUN):
            start = pos_ref[block * tok + r * RUN] + index - r * RUN
            value = jnp.where(index >= r * RUN, start, value)
        return value

    own_pos = run_positions(me, row)
    query_pos = jnp.concatenate([own_pos] * heads, axis=0)
    step_blocks = min(n, 8)
    span = step_blocks * tok

    def keys(c, which):
        return kv_all[pl.ds(c * step_blocks, step_blocks), which].reshape(span, HD)

    def loop(body, init):
        if n == step_blocks:
            return body(0, init)
        return lax.fori_loop(0, n // step_blocks, body, init)

    def at(c):
        return pl.ds(c * span if isinstance(c, int) else pl.multiple_of(c * span, span), span)

    def score_step(c, top):
        value = lax.dot_general(
            query, keys(c, 0), (((1,), (1,)), ((), ())), preferred_element_type=jnp.float32
        )
        key_pos = jnp.concatenate(
            [run_positions(c * step_blocks + b, lane) for b in range(step_blocks)], axis=1
        )
        value = jnp.where(key_pos <= query_pos, value * scale, BIG_NEGATIVE)
        scores[:, at(c)] = value
        return jnp.maximum(top, jnp.max(value, axis=1, keepdims=True))

    top = loop(score_step, jnp.full((total_rows, 1), BIG_NEGATIVE, jnp.float32))

    def out_step(c, carry):
        norm, out = carry
        weights = jnp.exp(scores[:, at(c)] - top)
        scores[:, at(c)] = weights
        norm = norm + jnp.sum(weights, axis=1, keepdims=True)
        out = out + jnp.dot(
            weights.astype(jnp.bfloat16), keys(c, 1), preferred_element_type=jnp.float32
        )
        return norm, out

    norm, out = loop(
        out_step,
        (jnp.zeros((total_rows, 1), jnp.float32), jnp.zeros((total_rows, HD), jnp.float32)),
    )
    inverse = 1.0 / norm
    attn = out * inverse
    for h in range(heads):
        attn_own[:, pl.ds(h * HD, HD)] = attn[h * tok : (h + 1) * tok].astype(jnp.bfloat16)
    at_gather = Gather(n, me, attn_own, attn_all, at_send, at_relay, at_recv)
    at_gather.start()

    grad = part[hme].astype(jnp.float32)
    for k in range(1, m):
        src = lax.rem(hme + k, m)
        remote(
            part.at[0], part_all.at[src], p_send.at[k], p_recv.at[src], "head", src
        ).wait_recv()
        grad = grad + part_all[src].astype(jnp.float32)
    grad = jnp.concatenate(
        [grad[:, h * HD : (h + 1) * HD] for h in range(heads)], axis=0
    ).astype(jnp.bfloat16)
    delta = jnp.sum(grad.astype(jnp.float32) * attn, axis=1, keepdims=True)

    def grad_step(c, total):
        dprob = lax.dot_general(
            grad, keys(c, 1), (((1,), (1,)), ((), ())), preferred_element_type=jnp.float32
        )
        dscore = (scores[:, at(c)] * inverse * (dprob - delta)).astype(jnp.bfloat16)
        return total + jnp.dot(dscore, keys(c, 0), preferred_element_type=jnp.float32)

    d_rows = loop(grad_step, jnp.zeros((total_rows, HD), jnp.float32)) * scale
    for h in range(heads):
        dq_ref[:, pl.ds(h * HD, HD)] = d_rows[h * tok : (h + 1) * tok].astype(jnp.bfloat16)

    total = jnp.dot(g_block(me)[...], attn_own[...], preferred_element_type=jnp.float32)

    def g_arrived(src):
        remote(
            g_block(me), g_all.at[src], g_send.at[1], g_recv.at[src], "seq", src
        ).wait_recv()

    for k in range(1, n // 2):
        at_gather.pass_on(k)
    order = [at_gather.other(0)]
    for k in range(1, n // 2):
        order += [at_gather.peer(k), at_gather.other(k)]
    for index, src in enumerate(order):
        if index % 2 == 0:
            at_gather.arrived(src)
        g_arrived(src)
        total = total + jnp.dot(g_all[src], attn_all[src], preferred_element_type=jnp.float32)
    for h in range(heads):
        dw_ref[h] = total[:, h * HD : (h + 1) * HD]

    kv.finish()
    at_gather.finish()
    for k in range(1, n):
        g_send_copy(k).wait_send()
    for k in range(1, m):
        p_copy(k).wait_send()


def body(n, m, queries, keys_values, out_weight, out_grad, positions):
    tok, width = queries.shape
    heads = width // HD
    dz, all_heads, _ = out_weight.shape
    features = out_grad.shape[1]
    rows = features // n
    turn = rows % 16 == 0 and dz % HD == 0 and features % HD == 0
    bf16, f32 = jnp.bfloat16, jnp.float32
    if not turn:
        out_grad = out_grad.T.reshape(n, rows, tok)
    vmem = pl.BlockSpec(memory_space=pltpu.VMEM)
    anywhere = pl.BlockSpec(memory_space=pl.ANY)
    dma = pltpu.SemaphoreType.DMA
    d_query, d_weight = pl.pallas_call(
        functools.partial(kernel, n, m, turn),
        out_shape=(
            jax.ShapeDtypeStruct((tok, width), bf16),
            jax.ShapeDtypeStruct((heads, rows, HD), f32),
        ),
        in_specs=[
            pl.BlockSpec(memory_space=pltpu.SMEM),
            vmem,
            vmem,
            anywhere,
            anywhere,
        ],
        out_specs=(vmem, vmem),
        scratch_shapes=[
            pltpu.VMEM(out_grad.shape, bf16),
            pltpu.VMEM((features, tok) if turn else (16, HD), bf16),
            pltpu.VMEM(out_weight.shape, bf16),
            pltpu.VMEM((n, 2, tok, HD), bf16),
            pltpu.VMEM((m, tok, width), bf16),
            pltpu.VMEM((tok, width), f32),
            pltpu.VMEM((m, tok, width), bf16),
            pltpu.VMEM((tok, width), bf16),
            pltpu.VMEM((n, tok, width), bf16),
            pltpu.VMEM((n, rows, tok), bf16),
            pltpu.VMEM((heads * tok, n * tok), f32),
            dma((2,)),
            dma((n,)),
            dma((n,)),
            dma((n,)),
            dma((n,)),
            dma((n,)),
            dma((n,)),
            dma((n,)),
            dma((n,)),
            dma((m,)),
            dma((m,)),
        ],
        compiler_params=pltpu.CompilerParams(
            collective_id=0, has_side_effects=True, vmem_limit_bytes=56 * 1024 * 1024
        ),
    )(positions, queries, keys_values, out_grad, out_weight)
    return d_query, d_weight.transpose(1, 0, 2)


def solution(mesh):
    n, m = mesh.shape["seq"], mesh.shape["head"]
    return jax.shard_map(
        functools.partial(body, n, m),
        mesh=mesh,
        in_specs=(
            P("seq", "head"),
            P(None, "seq", None),
            P("head", None, None),
            P("seq", None),
            P(),
        ),
        out_specs=(P("seq", "head"), P("seq", "head", None)),
        check_vma=False,
    )
```

time: 125 us -> 27.8 us (0.22)
  waiting for transfers between devices: 79.7 us -> 0 us
  Pallas kernels: 0 us -> 23.5 us
  between operations: 14.8 us -> 0.64 us
  blocking collectives: 10.7 us -> 0 us
  local copies, waits for them, and re-layouts: 10.1 us -> 3.42 us
  starting transfers between devices: 5.54 us -> 0 us
  matrix products: 2.08 us -> 0 us
    unnamed x2 -> x0, waiting for transfers between devices: 60.9 us -> none
    pallas_call x0 -> x1, Pallas kernels: none -> 23.5 us  [body(): pl.pallas_call(functools.partial(kernel, n, m, turn), out_shape=(jax.Shap...]
    all_to_all x1 -> x0, waiting for transfers between devices: 18.8 us -> none  [body(): lax.all_to_all(out_weight, 'head', split_axis=1, concat_axis=0, tiled=True)]
    all_gather x1 -> x0, blocking collectives: 10.7 us -> none  [body(): all_kv = lax.all_gather(own_kv, 'seq', axis=1, tiled=True)]
    all_to_all x1 -> x0, starting transfers between devices: 5.54 us -> none  [body(): lax.all_to_all(out_weight, 'head', split_axis=1, concat_axis=0, tiled=True)]
    dot_general x1 -> x0, local copies, waits for them, and re-layouts: 3.14 us -> none  [body(): jnp.einsum('td,thc->dhc', out_grad, attn, preferred_element_type=jnp.floa...]
    unnamed x25 -> x2, local copies, waits for them, and re-layouts: 5.82 us -> 3.42 us
    dot_general x5 -> x0, matrix products: 2.08 us -> none  [the longest x1 0.52 us: body(): jnp.einsum('td,thc->dhc', out_grad, attn, preferred_element_type=jnp.floa...]
  transfers between devices with their start and end apart: 2 -> 0, of which waited for: 2 -> 0; matrix products, arithmetic and copies ran while one was open for 3% -> 0% of each run, Pallas kernels for 0% -> 0%
where the time goes in v1:
time: 27.8 us; the launch traced here: 27.6 us
  Pallas kernels  23.5 us (85%)
  local copies, waits for them, and re-layouts  3.42 us (12%)
  between operations  0.64 us (2%)
    pallas_call x1, Pallas kernels, body(): pl.pallas_call(functools.partial(kernel, n, m, turn), out_shape=(jax.Shap...  23.5 us
    unnamed x2, local copies, waits for them, and re-layouts  3.42 us

profile of v1, /device:TPU:1, one launch (start us, length us, event | category | flops | bytes accessed | tf_op | source)
XLA Modules:
  0.0 27.6 jit_solution(10493712486263992859)
XLA Ops:
  0.6 23.5 %shard_map.68 = (bf16[128,256]{1,0:T(8,128)(2,1)}, f32[2,320,128]{2,1,0:T(8,128)}) custom-call(s32[1024]{0:T(1024)} %pos_ref.1, bf16[128,256]{1,0:T(8,128)(2,1)} %q_ref.1, bf16[2,128,128]{2,1,0:T(8,128)(2,1)} %kv_ref.1, bf16[128,2560]{1,0:T(8,128)(2,1)} %g_hbm.1, bf16[640,8,128]{2,1,0:T(8,128)(2,1)} %w_hbm.1), custom_call_target="tpu_custom_call" | custom-call | tf_op jit(solution)/shard_map/pallas_call | solution.py:332
  24.2 2.0 %copy.7 = f32[320,2,128]{2,1,0:T(2,128)} copy(f32[320,2,128]{2,0,1:T(8,128)} %bitcast.1) | data formatting | bytes 655360
  26.1 1.5 %copy.9 = bf16[128,256]{1,0:T(8,128)(2,1)} copy(bf16[128,256]{1,0:T(8,128)(2,1)} %get-tuple-element.10) | data formatting | bytes 131072

commit v2 on v1

--- a/solution.py
+++ b/solution.py
@@ -10,6 +10,7 @@
 HD = 128
 GROUP = 8
 RUN = 64
+VMEM_LIMIT = 67043328
 BIG_NEGATIVE = -1e30
 MESH = pl.DeviceIdType.MESH
 
@@ -81,19 +82,21 @@
     n,
     m,
     turn,
-    pos_ref,
-    q_ref,
-    kv_ref,
+    pos_hbm,
+    q_hbm,
+    kv_hbm,
     g_hbm,
     w_hbm,
     dq_ref,
     dw_ref,
+    pos_ref,
+    q_ref,
+    kv_ref,
     g_v,
     gt_v,
     w_v,
     kv_all,
     part,
-    part_own,
     part_all,
     attn_own,
     attn_all,
@@ -119,11 +122,6 @@
     dz = w_v.shape[0]
     scale = HD ** (-0.5)
 
-    g_copy = pltpu.make_async_copy(g_hbm, g_v, local_sem.at[0])
-    w_copy = pltpu.make_async_copy(w_hbm, w_v, local_sem.at[1])
-    g_copy.start()
-    w_copy.start()
-
     barrier = pltpu.get_barrier_semaphore()
     for k in range(1, n):
         pl.semaphore_signal(
@@ -133,14 +131,19 @@
         pl.semaphore_signal(
             barrier, inc=1, device_id={"head": lax.rem(hme + k, m)}, device_id_type=MESH
         )
-    pl.semaphore_wait(barrier, n + m - 2)
 
     group = lax.div(hme * heads, GROUP)
     columns = pl.ds(pl.multiple_of(group * HD, HD), HD)
-    own_kv = kv_ref.at[:, :, columns]
-    kv = Gather(n, me, own_kv, kv_all, kv_send, kv_relay, kv_recv)
-    kv.start()
-    kv_all[me] = own_kv[...]
+    own_kv = kv_ref.at[...]
+    kv_copy = pltpu.make_async_copy(kv_hbm.at[:, :, columns], kv_ref, local_sem.at[0])
+    g_copy = pltpu.make_async_copy(g_hbm, g_v, local_sem.at[1])
+    w_copy = pltpu.make_async_copy(w_hbm, w_v, local_sem.at[2])
+    q_copy = pltpu.make_async_copy(q_hbm, q_ref, local_sem.at[3])
+    pos_copy = pltpu.make_async_copy(pos_hbm, pos_ref, local_sem.at[4])
+    for copy in (kv_copy, g_copy, w_copy, q_copy, pos_copy):
+        copy.start()
+    kv_copy.wait()
+    kv_all[me] = kv_ref[...]
 
     g_copy.wait()
     if turn:
@@ -154,6 +157,10 @@
 
         def g_block(i):
             return g_v.at[i]
+
+    pl.semaphore_wait(barrier, n + m - 2)
+    kv = Gather(n, me, own_kv, kv_all, kv_send, kv_relay, kv_recv)
+    kv.start()
 
     def g_send_copy(k):
         to = lax.rem(me + k, n)
@@ -203,6 +210,8 @@
     for k in range(n // 2):
         kv.arrived(kv.other(k))
 
+    q_copy.wait()
+    pos_copy.wait()
     query = jnp.concatenate([q_ref[:, pl.ds(h * HD, HD)] for h in range(heads)], axis=0)
     total_rows = heads * tok
     row = lax.broadcasted_iota(jnp.int32, (tok, 1), 0)
@@ -244,22 +253,21 @@
 
     top = loop(score_step, jnp.full((total_rows, 1), BIG_NEGATIVE, jnp.float32))
 
-    def out_step(c, carry):
-        norm, out = carry
+    def norm_step(c, norm):
         weights = jnp.exp(scores[:, at(c)] - top)
         scores[:, at(c)] = weights
-        norm = norm + jnp.sum(weights, axis=1, keepdims=True)
-        out = out + jnp.dot(
-            weights.astype(jnp.bfloat16), keys(c, 1), preferred_element_type=jnp.float32
-        )
-        return norm, out
-
-    norm, out = loop(
-        out_step,
-        (jnp.zeros((total_rows, 1), jnp.float32), jnp.zeros((total_rows, HD), jnp.float32)),
-    )
-    inverse = 1.0 / norm
-    attn = out * inverse
+        return norm + jnp.sum(weights, axis=1, keepdims=True)
+
+    inverse = 1.0 / loop(norm_step, jnp.zeros((total_rows, 1), jnp.float32))
+
+    def out_step(c, out):
+        probs = scores[:, at(c)] * inverse
+        scores[:, at(c)] = probs
+        return out + jnp.dot(
+            probs.astype(jnp.bfloat16), keys(c, 1), preferred_element_type=jnp.float32
+        )
+
+    attn = loop(out_step, jnp.zeros((total_rows, HD), jnp.float32))
     for h in range(heads):
         attn_own[:, pl.ds(h * HD, HD)] = attn[h * tok : (h + 1) * tok].astype(jnp.bfloat16)
     at_gather = Gather(n, me, attn_own, attn_all, at_send, at_relay, at_recv)
@@ -281,7 +289,7 @@
         dprob = lax.dot_general(
             grad, keys(c, 1), (((1,), (1,)), ((), ())), preferred_element_type=jnp.float32
         )
-        dscore = (scores[:, at(c)] * inverse * (dprob - delta)).astype(jnp.bfloat16)
+        dscore = (scores[:, at(c)] * (dprob - delta)).astype(jnp.bfloat16)
         return total + jnp.dot(dscore, keys(c, 0), preferred_element_type=jnp.float32)
 
     d_rows = loop(grad_step, jnp.zeros((total_rows, HD), jnp.float32)) * scale
@@ -316,6 +324,12 @@
         p_copy(k).wait_send()
 
 
+def place(dq_in, dw_in, dq_ref, dw_ref):
+    dq_ref[...] = dq_in[...]
+    for h in range(dw_in.shape[0]):
+        dw_ref[:, h, :] = dw_in[h]
+
+
 def body(n, m, queries, keys_values, out_weight, out_grad, positions):
     tok, width = queries.shape
     heads = width // HD
@@ -327,35 +341,35 @@
     if not turn:
         out_grad = out_grad.T.reshape(n, rows, tok)
     vmem = pl.BlockSpec(memory_space=pltpu.VMEM)
-    anywhere = pl.BlockSpec(memory_space=pl.ANY)
+    anywhere = pl.BlockSpec(memory_space=pltpu.HBM)
     dma = pltpu.SemaphoreType.DMA
+    buffers = [
+        pltpu.VMEM((tok, width), bf16),
+        pltpu.VMEM((2, tok, HD), bf16),
+        pltpu.VMEM(out_grad.shape, bf16),
+        pltpu.VMEM((features, tok) if turn else (16, HD), bf16),
+        pltpu.VMEM(out_weight.shape, bf16),
+        pltpu.VMEM((n, 2, tok, HD), bf16),
+        pltpu.VMEM((m, tok, width), bf16),
+        pltpu.VMEM((m, tok, width), bf16),
+        pltpu.VMEM((tok, width), bf16),
+        pltpu.VMEM((n, tok, width), bf16),
+        pltpu.VMEM((n, rows, tok), bf16),
+        pltpu.VMEM((heads * tok, n * tok), f32),
+    ]
+    results = 2 * tok * width + 4 * rows * width
     d_query, d_weight = pl.pallas_call(
         functools.partial(kernel, n, m, turn),
         out_shape=(
             jax.ShapeDtypeStruct((tok, width), bf16),
             jax.ShapeDtypeStruct((heads, rows, HD), f32),
         ),
-        in_specs=[
-            pl.BlockSpec(memory_space=pltpu.SMEM),
-            vmem,
-            vmem,
-            anywhere,
-            anywhere,
-        ],
+        in_specs=[anywhere] * 5,
         out_specs=(vmem, vmem),
         scratch_shapes=[
-            pltpu.VMEM(out_grad.shape, bf16),
-            pltpu.VMEM((features, tok) if turn else (16, HD), bf16),
-            pltpu.VMEM(out_weight.shape, bf16),
-            pltpu.VMEM((n, 2, tok, HD), bf16),
-            pltpu.VMEM((m, tok, width), bf16),
-            pltpu.VMEM((tok, width), f32),
-            pltpu.VMEM((m, tok, width), bf16),
-            pltpu.VMEM((tok, width), bf16),
-            pltpu.VMEM((n, tok, width), bf16),
-            pltpu.VMEM((n, rows, tok), bf16),
-            pltpu.VMEM((heads * tok, n * tok), f32),
-            dma((2,)),
+            pltpu.SMEM(positions.shape, jnp.int32),
+            *buffers,
+            dma((5,)),
             dma((n,)),
             dma((n,)),
             dma((n,)),
@@ -368,10 +382,20 @@
             dma((m,)),
         ],
         compiler_params=pltpu.CompilerParams(
-            collective_id=0, has_side_effects=True, vmem_limit_bytes=56 * 1024 * 1024
+            collective_id=0, has_side_effects=True, vmem_limit_bytes=VMEM_LIMIT - results - (24 << 10)
         ),
     )(positions, queries, keys_values, out_grad, out_weight)
-    return d_query, d_weight.transpose(1, 0, 2)
+    return pl.pallas_call(
+        place,
+        out_shape=(
+            jax.ShapeDtypeStruct((tok, width), bf16),
+            jax.ShapeDtypeStruct((rows, heads, HD), f32),
+        ),
+        in_specs=[vmem, vmem],
+        out_specs=(vmem, vmem),
+        compiler_params=pltpu.CompilerParams(vmem_limit_bytes=4 << 20),
+        cost_estimate=pl.CostEstimate(flops=1 << 20, bytes_accessed=1 << 20, transcendentals=0),
+    )(d_query, d_weight)
 
 
 def solution(mesh):

time: 27.8 us -> 26.3 us (0.946)
  local copies, waits for them, and re-layouts: 3.42 us -> 1.8 us
    unnamed x2 -> x4, local copies, waits for them, and re-layouts: 3.42 us -> 1.8 us
    pallas_call x0 -> x1, Pallas kernels: none -> 0.91 us  [body(): pl.pallas_call(place, out_shape=(jax.ShapeDtypeStruct((tok, width), bf16)...]
    pallas_call x1, Pallas kernels: 23.5 us -> 22.7 us  [body(): pl.pallas_call(functools.partial(kernel, n, m, turn), out_shape=(jax.Shap...]
where the time goes in v2:
time: 26.3 us; the launch traced here: 26.1 us
  Pallas kernels  23.6 us (90%)
  local copies, waits for them, and re-layouts  1.8 us (7%)
  between operations  0.65 us (2%)
    pallas_call x1, Pallas kernels, body(): pl.pallas_call(functools.partial(kernel, n, m, turn), out_shape=(jax.Shap...  22.7 us
    unnamed x4, local copies, waits for them, and re-layouts  1.8 us
    pallas_call x1, Pallas kernels, body(): pl.pallas_call(place, out_shape=(jax.ShapeDtypeStruct((tok, width), bf16)...  0.91 us

profile of v2, /device:TPU:1, one launch (start us, length us, event | category | flops | bytes accessed | tf_op | source)
XLA Modules:
  0.0 26.1 jit_solution(12261200605309954729)
XLA Ops:
  0.6 22.7 %shard_map.68 = (bf16[128,256]{1,0:T(8,128)(2,1)}, f32[2,320,128]{2,1,0:T(8,128)}) custom-call(s32[1024]{0:T(1024)} %pos_hbm.1, bf16[128,256]{1,0:T(8,128)(2,1)} %q_hbm.1, bf16[2,128,128]{2,1,0:T(8,128)(2,1)} %kv_hbm.1, bf16[128,2560]{1,0:T(8,128)(2,1)} %g_hbm.1, bf16[640,8,128]{2,1,0:T(8,128)(2,1)} %w_hbm.1), custom_call_target="tpu_custom_call" | custom-call | tf_op jit(solution)/shard_map/pallas_call | solution.py:361
  23.3 0.0 copy-start
  23.3 1.0 %copy-done = f32[2,320,128]{2,1,0:T(8,128)S(1)} copy-done((f32[2,320,128]{2,1,0:T(8,128)S(1)}, f32[2,320,128]{2,1,0:T(8,128)}, u32[]{:S(2)}) %copy-start) | copy-done | bytes 327704
  24.3 0.0 copy-start.1
  24.3 0.8 %copy-done.1 = bf16[128,256]{1,0:T(8,128)(2,1)S(1)} copy-done((bf16[128,256]{1,0:T(8,128)(2,1)S(1)}, bf16[128,256]{1,0:T(8,128)(2,1)}, u32[]{:S(2)}) %copy-start.1) | copy-done | bytes 65560
  25.1 0.9 %shard_map.69 = (bf16[128,256]{1,0:T(8,128)(2,1)}, f32[320,2,128]{2,1,0:T(2,128)}) custom-call(bf16[128,256]{1,0:T(8,128)(2,1)S(1)} %copy-done.1, f32[2,320,128]{2,1,0:T(8,128)S(1)} %copy-done), custom_call_target="tpu_custom_call" | custom-call | flops 1048576 | bytes 1048576 | tf_op jit(solution)/shard_map/pallas_call | solution.py:388
Async XLA Ops:
  23.3 1.0 %copy-start = (f32[2,320,128]{2,1,0:T(8,128)S(1)}, f32[2,320,128]{2,1,0:T(8,128)}, u32[]{:S(2)}) copy-start(f32[2,320,128]{2,1,0:T(8,128)} %get-tuple-element.5.dw_in) | copy-start | bytes 983044
  24.3 0.8 %copy-start.1 = (bf16[128,256]{1,0:T(8,128)(2,1)S(1)}, bf16[128,256]{1,0:T(8,128)(2,1)}, u32[]{:S(2)}) copy-start(bf16[128,256]{1,0:T(8,128)(2,1)} %get-tuple-element.4.dq_in) | copy-start | bytes 196612
